TPU v7x, 128 devices: a whole 4x4x4 slice. The times are simulated.
128 devices in a mesh: slab: 32 (over y, x, core), orb: 4 (over z).
Axes of the slice: x: 4, y: 4, z: 4, core: 2. Of those that a mesh axis runs over, the one named last changes fastest.
Arguments:
- orbitals: float32 [256, 64, 4096], P('orb', 'slab'), may hold values from -6 to 6
- pair_list: int32 [128, 2], P(('slab', 'orb')), may hold values from 0 to 255, as said below
- box_start: int32 [128, 3], P(('slab', 'orb')), may hold values from 0 to 63
Outputs:
- exchange_action: float32 [256, 64, 4096], P('orb', 'slab')
Inputs may be any that keep to these rules, and one draw needn't show every extreme that they name: `pair_list`: the two orbitals of a row differ.
All inputs are finite; a program needn't handle non-finite values.
Results may differ from a plain program's by a relative error of at most 0.0003.
Values sent between devices are 32-bit elements; how exact they have to be, the bound alone decides.
A program may use at most 128 MiB of HBM per device.

v0:
```python
import jax
import jax.numpy as jnp
from jax import lax
from jax.sharding import PartitionSpec as P

NX = 64
NY = 64
NZ = 64
ITERS = 16
screening = 0.02
center_eig = 6.0 + screening
half_width = 6.0
sigma_one = center_eig / half_width


def side_by_side(arrays, axis, dim, along):
    ends, at = ([], 0)
    for a in arrays[:-1]:
        at += a.shape[along]
        ends.append(at)
    both = jnp.concatenate(arrays, axis=along)
    return tuple(jnp.split(lax.all_gather(both, axis, axis=dim, tiled=True), ends, axis=along))


def operate(field):
    cells = field.shape[2]
    z_index = jnp.arange(cells, dtype=jnp.int32) % NZ
    beside = jnp.roll(field, 1, 1) + jnp.roll(field, -1, 1)
    beside = beside + jnp.roll(field, NZ, 2) + jnp.roll(field, -NZ, 2)
    upper = jnp.where(z_index == NZ - 1, jnp.roll(field, NZ - 1, 2), jnp.roll(field, -1, 2))
    lower = jnp.where(z_index == 0, jnp.roll(field, 1 - NZ, 2), jnp.roll(field, 1, 2))
    return center_eig * field - (beside + upper + lower)


def solve_screened(density):

    def sweep(step_index, state_now):
        solution, residue, update, ratio = state_now
        solution = solution + update
        residue = residue - operate(update)
        ratio_next = 1.0 / (2.0 * sigma_one - ratio)
        update = ratio_next * ratio * update + 2.0 * ratio_next / half_width * residue
        return (solution, residue, update, ratio_next)

    start_state = (
        jnp.zeros_like(density),
        density,
        density / center_eig,
        jnp.asarray(1.0 / sigma_one, jnp.float32),
    )
    return lax.fori_loop(0, ITERS, sweep, start_state)[0]


def pair_work(received):
    left = received[:, 0]
    right = received[:, 1]
    potential = solve_screened(left * right)
    return jnp.stack([-potential * right, -potential * left], axis=1)


def box_mask(starts, slab_at, slab_rows, cells):
    x_cells = slab_at * slab_rows + jnp.arange(slab_rows, dtype=jnp.int32)
    cell_index = jnp.arange(cells, dtype=jnp.int32)
    y_index = cell_index // NZ
    z_index = cell_index % NZ
    inside_x = (x_cells[None, None, :] - starts[:, :, 0:1]) % NX < NX // 2
    inside_y = (y_index[None, None, :] - starts[:, :, 1:2]) % NY < NY // 2
    inside_z = (z_index[None, None, :] - starts[:, :, 2:3]) % NZ < NZ // 2
    inside = inside_x[:, :, :, None] & (inside_y & inside_z)[:, :, None, :]
    return inside[:, None]


def body(orbitals, pair_list, box_start):
    n_slab = lax.axis_size("slab")
    n_orb = lax.axis_size("orb")
    slab_at = lax.axis_index("slab")
    orb_at = lax.axis_index("orb")
    orb_dev, slab_rows, cells = orbitals.shape
    pair_dev = pair_list.shape[0]
    devices = n_slab * n_orb
    all_pairs, all_boxes = side_by_side((pair_list, box_start), ("slab", "orb"), 0, 1)
    pair_grid = all_pairs.reshape(n_slab, n_orb, pair_dev, 2)
    box_grid = all_boxes.reshape(n_slab, n_orb, pair_dev, 3)
    row_pairs = jnp.take(pair_grid, orb_at, axis=1).transpose(1, 2, 0)
    own_y = jnp.broadcast_to(box_start[:, None, 1:2], (pair_dev, 2, 1)).reshape(-1)
    own_z = jnp.broadcast_to(box_start[:, None, 2:3], (pair_dev, 2, 1)).reshape(-1)
    boxed_frame = False
    gathered = lax.all_gather(orbitals, "orb", axis=0, tiled=True)
    starts = jnp.take(box_grid, orb_at, axis=1).transpose(1, 0, 2)
    pieces = jnp.take(gathered, row_pairs, axis=0)
    pieces = jnp.where(box_mask(starts, slab_at, slab_rows, cells), pieces, 0.0)
    outgoing = pieces.reshape(pair_dev, 2, n_slab * slab_rows, cells)
    terms = pair_work(lax.all_to_all(outgoing, "slab", split_axis=2, concat_axis=2, tiled=True))
    full_rows = n_slab * slab_rows
    spread = jnp.broadcast_to(
        terms.reshape(pair_dev, 2, n_slab, 1, slab_rows, cells),
        (pair_dev, 2, n_slab, n_orb, slab_rows, cells),
    )
    spread = spread.reshape(pair_dev, 2, devices * slab_rows, cells)
    returned = lax.all_to_all(spread, ("slab", "orb"), split_axis=2, concat_axis=2, tiled=True)
    owners = (
        all_pairs.reshape(devices, pair_dev, 2).transpose(1, 2, 0).reshape(-1) - orb_at * orb_dev
    )
    one_hot = (jnp.arange(orb_dev, dtype=jnp.int32)[:, None] == owners[None, :]).astype(jnp.float32)
    action = jnp.dot(
        one_hot,
        returned.reshape(pair_dev * 2 * devices, slab_rows * cells),
        precision=lax.Precision.HIGHEST,
        preferred_element_type=jnp.float32,
    )
    return action.reshape(orb_dev, slab_rows, cells)


def solution(mesh):
    return jax.shard_map(
        body,
        mesh=mesh,
        in_specs=(P("orb", "slab", None), P(("slab", "orb"), None), P(("slab", "orb"), None)),
        out_specs=P("orb", "slab", None),
        check_vma=False,
    )
```

profile of v0, /device:TPU:1, one launch (start us, length us, event | category | flops | bytes accessed | tf_op | source)
XLA Modules:
  0.0 380.7 jit_solution(14061761828574327259)
XLA Ops:
  7.4 50.4 %all-gather = s32[128,1,5]{2,1,0:T(1,128)S(1)} all-gather(s32[1,1,5]{2,1,0:T(1,128)S(1)} %add_bitcast_fusion), channel_id=1, replica_groups=mesh['slab'=32,'orb'=4] {'slab','orb'}, dimensions={0}, use_global_device_ids=true | all-gather | bytes 2580 | tf_op jit(solution)/shard_map/all_gather | solution.py:22
  60.8 35.6 %all-gather.3.cloned.1.call-done = f32[256,2,4096]{2,1,0:T(2,128)} async-done(((f32[64,2,4096]{2,1,0:T(2,128)}), f32[256,2,4096]{2,1,0:T(2,128)}) %all-gather.3.cloned.1.call-update) | async-done | bytes 8388624 | tf_op jit(solution)/shard_map/all_gather | solution.py:88
  96.4 6.2 %gather_fusion = f32[64,2,4096]{2,1,0:T(2,128)S(1)} fusion(f32[256,2,4096]{2,1,0:T(2,128)} %all-gather.3.cloned.1.call-done, s32[1024]{0:T(1024)S(1)} %pad_clamp_fusion), kind=kCustom, calls=%fused_computation | custom fusion | bytes 4194560 | tf_op jit(solution)/shard_map/jit(_take)/gather | solution.py:90
  102.6 2.4 gather.17
  105.0 5.6 %fusion.11 = f32[1,2,64,4096]{3,1,0,2:T(2,128)} fusion(f32[1,2,64,4096]{3,2,1,0:T(8,128)} %gather.17, pred[2,64]{0,1:T(8,128)(4,1)S(1)} %copy.15, pred[64,4096]{1,0:T(8,128)(4,1)S(1)} %broadcast_and_fusion), kind=kLoop, calls=%fused_computation.22 | loop fusion | flops 1048576 | bytes 4456576 | tf_op jit(solution)/shard_map/jit(_where)/select_n | solution.py:91
  110.6 7.7 %all-to-all-start = ((f32[1,2,64,4096]{3,1,0,2:T(2,128)}), f32[1,2,64,4096]{3,1,0,2:T(2,128)S(1)}, u32[]{:S(2)}, u32[]{:S(2)}) async-start(f32[1,2,64,4096]{3,1,0,2:T(2,128)} %fusion.11), calls=%async_computation | async-start | bytes 4194304 | tf_op jit(solution)/shard_map/all_to_all | solution.py:93
  118.4 28.5 %all-to-all-done = f32[1,2,64,4096]{3,1,0,2:T(2,128)S(1)} async-done(((f32[1,2,64,4096]{3,1,0,2:T(2,128)}), f32[1,2,64,4096]{3,1,0,2:T(2,128)S(1)}, u32[]{:S(2)}, u32[]{:S(2)}) %all-to-all-start) | async-done | bytes 2097184 | tf_op jit(solution)/shard_map/all_to_all | solution.py:93
  146.9 2.3 broadcast_multiply_fusion
  150.5 54.3 %while.19 = (s32[]{:T(128)}, f32[1,64,4096]{2,1,0:T(8,128)S(1)}, f32[1,64,4096]{2,1,0:T(8,128)S(1)}, f32[1,64,4096]{2,1,0:T(8,128)S(1)}, f32[]{:T(128)}, /*index...) while((s32[]{:T(128)}, f32[1,64,4096]{2,1,0:T(8,128)S(1)}, ...), condition=%wide.region_1.2_spmd.clone, body=%wide.region_0.1_spmd.clone.sunk | while | flops 6062087 | bytes 32522416 | solution.py:51
  152.4 1.5 multiply_add_fusion.2
  159.2 1.5 multiply_add_fusion.2
  166.0 1.5 multiply_add_fusion.2
  172.7 1.5 multiply_add_fusion.2
  204.8 5.3 %fusion.14 = (f32[1,64,4096]{2,0,1:T(1,128)S(1)}, f32[1,64,4096]{2,0,1:T(1,128)S(1)}) fusion(f32[1,2,64,4096]{3,1,0,2:T(2,128)} %copy-done, f32[1,64,4096]{2,1,0:T(8,128)S(1)} %get-tuple-element.32), kind=kLoop, calls=%fused_computation.38 | loop fusion | flops 786432 | bytes 5242880 | tf_op jit(solution)/shard_map/mul | solution.py:58
  210.1 4.0 %pad_maximum_fusion = f32[1,2,32,1,2,4096]{5,0,4,3,2,1:T(1,128)S(1)} fusion(f32[1,1,32,1,2,4096]{5,0,4,3,2,1:T(1,128)S(1)} %bitcast.60, f32[1,1,32,1,2,4096]{5,0,4,3,2,1:T(1,128)S(1)} %bitcast.59), kind=kLoop, calls=%fused_computation.19 | loop fusion | flops 524288 | bytes 4194304 | tf_op jit(solution)/shard_map/stack | solution.py:58
  214.1 1.9 copy.38
  216.0 7.5 %broadcast_in_dim.91 = f32[2,32,4,2,4096]{4,0,3,2,1:T(2,128)} broadcast(f32[2,32,2,4096]{3,0,2,1:T(2,128)S(1)} %bitcast.58), dimensions={0,1,3,4} | broadcast | bytes 10485760 | tf_op jit(solution)/shard_map/broadcast_in_dim | solution.py:95
  223.5 6.4 %all-to-all-start.1 = ((f32[1,2,256,4096]{3,1,0,2:T(2,128)}), f32[1,2,256,4096]{3,1,0,2:T(2,128)}, u32[]{:S(2)}, u32[]{:S(2)}) async-start(f32[1,2,256,4096]{3,1,0,2:T(2,128)} %bitcast.55), calls=%async_computation.1 | async-start | bytes 16777216 | tf_op jit(solution)/shard_map/all_to_all | solution.py:100
  230.0 102.7 %all-to-all-done.1 = f32[1,2,256,4096]{3,1,0,2:T(2,128)} async-done(((f32[1,2,256,4096]{3,1,0,2:T(2,128)}), f32[1,2,256,4096]{3,1,0,2:T(2,128)}, u32[]{:S(2)}, u32[]{:S(2)}) %all-to-all-start.1) | async-done | bytes 8388640 | tf_op jit(solution)/shard_map/all_to_all | solution.py:100
  332.7 11.5 %copy.22 = f32[1,2,256,4096]{3,2,1,0:T(8,128)} copy(f32[1,2,256,4096]{3,1,0,2:T(2,128)} %all-to-all-done.1) | data formatting | bytes 16777216 | tf_op jit(solution)/shard_map/all_to_all | solution.py:100
  344.2 10.0 %reshape.587 = f32[256,8192]{1,0:T(8,128)} reshape(f32[1,2,256,4096]{3,2,1,0:T(8,128)} %copy.22) | data formatting | bytes 16777216 | tf_op jit(solution)/shard_map/reshape | solution.py:107
  354.2 9.0 %copy.23 = f32[8192,256]{1,0:T(8,128)} copy(f32[8192,256]{0,1:T(8,128)} %bitcast.57) | data formatting | bytes 16777216 | tf_op jit(solution)/shard_map/dot_general | solution.py:105
  363.2 7.7 %fusion.21 = f32[64,2,4096]{2,0,1:T(8,128)S(1)} fusion(f32[2,4096,256]{2,1,0:T(8,128)} %bitcast.56, s32[256]{0:T(256)S(1)} %bitcast.65), kind=kOutput, calls=%fused_computation.49 | convolution fusion | flops 1610629120 | bytes 10486784 | tf_op jit(solution)/shard_map/dot_general | solution.py:105
  370.9 2.9 copy.24
  (208 shorter events, 51.7 us)
Async XLA Ops:
  6.5 0.7 copy-start.1
  6.5 0.7 copy-start.2
  6.5 89.9 %all-gather.3.cloned.1.call-start = ((), (), s32[]{:S(2)}) async-start(), calls=%async_computation.2 | async-start | bytes 10485760 | tf_op jit(solution)/shard_map/all_gather | solution.py:88
  110.6 36.2 %all-to-all-start = ((f32[1,2,64,4096]{3,1,0,2:T(2,128)}), f32[1,2,64,4096]{3,1,0,2:T(2,128)S(1)}, u32[]{:S(2)}, u32[]{:S(2)}) async-start(f32[1,2,64,4096]{3,1,0,2:T(2,128)} %fusion.11), calls=%async_computation | async-start | bytes 4194304 | tf_op jit(solution)/shard_map/all_to_all | solution.py:93
  146.9 2.3 copy-start
  223.5 109.2 %all-to-all-start.1 = ((f32[1,2,256,4096]{3,1,0,2:T(2,128)}), f32[1,2,256,4096]{3,1,0,2:T(2,128)}, u32[]{:S(2)}, u32[]{:S(2)}) async-start(f32[1,2,256,4096]{3,1,0,2:T(2,128)} %bitcast.55), calls=%async_computation.1 | async-start | bytes 16777216 | tf_op jit(solution)/shard_map/all_to_all | solution.py:100
Sparse Core Ops, SparseCore 0:
  9.0 87.3 all-gather.2
where the time goes:
time: 382 us; the launch traced here: 381 us
  waiting for transfers between devices  168 us (44%)
  local copies, waits for them, and re-layouts  78.2 us (20%)
  blocking collectives  50.4 us (13%)
  other arithmetic  47.3 us (12%)
  starting transfers between devices  14.1 us (4%)
  between operations  13.6 us (4%)
  matrix products  7.74 us (2%)
    all_to_all x1, waiting for transfers between devices, body(): lax.all_to_all(spread, ('slab', 'orb'), split_axis=2, concat_axis=2, tile...  103 us
    all_gather x1, blocking collectives, side_by_side(): lax.all_gather(both, axis, axis=dim, tiled=True)  50.4 us
    all_gather x1, waiting for transfers between devices, body(): gathered = lax.all_gather(orbitals, 'orb', axis=0, tiled=True)  35.6 us
    all_to_all x1, waiting for transfers between devices, body(): lax.all_to_all(outgoing, 'slab', split_axis=2, concat_axis=2, tiled=True)  28.5 us
    add x16, other arithmetic, sweep(): ratio_next * ratio * update + 2.0 * ratio_next / half_width * residue  23.7 us
    dot_general x2, local copies, waits for them, and re-layouts, body(): jnp.dot(one_hot, returned.reshape(pair_dev * 2 * devices, slab_rows * cel...  11.9 us
    all_to_all x1, local copies, waits for them, and re-layouts, body(): lax.all_to_all(spread, ('slab', 'orb'), split_axis=2, concat_axis=2, tile...  11.5 us
    reshape x1, local copies, waits for them, and re-layouts, body(): returned.reshape(pair_dev * 2 * devices, slab_rows * cells)  9.99 us
  transfers between devices with their start and end apart: 3, of which 3 were waited for; matrix products, arithmetic and copies ran while one was open for 1% of the time, Pallas kernels for 0%

commit v1 on v0

--- a/solution.py
+++ b/solution.py
@@ -85,7 +85,13 @@
     own_y = jnp.broadcast_to(box_start[:, None, 1:2], (pair_dev, 2, 1)).reshape(-1)
     own_z = jnp.broadcast_to(box_start[:, None, 2:3], (pair_dev, 2, 1)).reshape(-1)
     boxed_frame = False
-    gathered = lax.all_gather(orbitals, "orb", axis=0, tiled=True)
+    current_arr = lax.all_to_all(
+        jnp.stack([orbitals for _ in range(lax.axis_size("orb"))]),
+        concat_axis=0,
+        split_axis=0,
+        axis_name="orb",
+    )
+    gathered = jnp.concatenate(current_arr, 0)
     starts = jnp.take(box_grid, orb_at, axis=1).transpose(1, 0, 2)
     pieces = jnp.take(gathered, row_pairs, axis=0)
     pieces = jnp.where(box_mask(starts, slab_at, slab_rows, cells), pieces, 0.0)

time: 382 us -> 427 us (1.12)
  blocking collectives: 50.4 us -> 133 us
  waiting for transfers between devices: 168 us -> 131 us
  between operations: 13.6 us -> 0.22 us
  local copies, waits for them, and re-layouts: 78.2 us -> 90.2 us
    all_gather x1, blocking collectives: 50.4 us -> 133 us  [side_by_side(): lax.all_gather(both, axis, axis=dim, tiled=True)]
    all_gather x1 -> x0, waiting for transfers between devices: 35.6 us -> none  [body(): gathered = lax.all_gather(orbitals, 'orb', axis=0, tiled=True)]
    another operation x0 -> x1, local copies, waits for them, and re-layouts: none -> 9.09 us  [body(): jnp.stack([orbitals for _ in range(lax.axis_size('orb'))])]
    all_to_all x0 -> x1, starting transfers between devices: none -> 5.98 us  [body(): lax.all_to_all(jnp.stack([orbitals for _ in range(lax.axis_size('orb'))])...]
  transfers between devices with their start and end apart: 3 -> 3, of which waited for: 3 -> 2; matrix products, arithmetic and copies ran while one was open for 1% -> 1% of each run, Pallas kernels for 0% -> 0%
where the time goes in v1:
time: 427 us; the launch traced here: 426 us
  blocking collectives  133 us (31%)
  waiting for transfers between devices  131 us (31%)
  local copies, waits for them, and re-layouts  90.2 us (21%)
  other arithmetic  43.4 us (10%)
  starting transfers between devices  17.8 us (4%)
  matrix products  7.74 us (2%)
    all_gather x1, blocking collectives, side_by_side(): lax.all_gather(both, axis, axis=dim, tiled=True)  133 us
    all_to_all x1, waiting for transfers between devices, body(): lax.all_to_all(spread, ('slab', 'orb'), split_axis=2, concat_axis=2, tile...  103 us
    all_to_all x1, waiting for transfers between devices, body(): lax.all_to_all(outgoing, 'slab', split_axis=2, concat_axis=2, tiled=True)  28.5 us
    add x16, other arithmetic, sweep(): ratio_next * ratio * update + 2.0 * ratio_next / half_width * residue  23.7 us
    dot_general x2, local copies, waits for them, and re-layouts, body(): jnp.dot(one_hot, returned.reshape(pair_dev * 2 * devices, slab_rows * cel...  11.9 us
    all_to_all x1, local copies, waits for them, and re-layouts, body(): lax.all_to_all(spread, ('slab', 'orb'), split_axis=2, concat_axis=2, tile...  11.5 us
    reshape x1, local copies, waits for them, and re-layouts, body(): returned.reshape(pair_dev * 2 * devices, slab_rows * cells)  9.98 us
    broadcast_in_dim x2, local copies, waits for them, and re-layouts, body(): jnp.broadcast_to(terms.reshape(pair_dev, 2, n_slab, 1, slab_rows, cells),...  9.4 us
  transfers between devices with their start and end apart: 3, of which 2 were waited for; matrix products, arithmetic and copies ran while one was open for 1% of the time, Pallas kernels for 0%

profile of v1, /device:TPU:1, one launch (start us, length us, event | category | flops | bytes accessed | tf_op | source)
XLA Modules:
  0.0 425.7 jit_solution(17376010108499345636)
XLA Ops:
  0.0 9.1 %stack.16 = f32[4,64,2,4096]{3,2,1,0:T(2,128)} broadcast(f32[64,2,4096]{2,1,0:T(2,128)} %param.5), dimensions={1,2,3} | broadcast | bytes 10485760 | tf_op jit(solution)/shard_map/stack | solution.py:89
  9.1 6.0 %all-to-all-start = ((f32[4,64,2,4096]{3,2,1,0:T(2,128)}), f32[4,64,2,4096]{3,2,1,0:T(2,128)}, u32[]{:S(2)}, u32[]{:S(2)}) async-start(f32[4,64,2,4096]{3,2,1,0:T(2,128)} %stack.16), calls=%async_computation | async-start | bytes 16777216 | tf_op jit(solution)/shard_map/all_to_all | solution.py:88
  15.2 133.3 %all-gather = s32[128,1,5]{2,1,0:T(1,128)S(1)} all-gather(s32[1,1,5]{2,1,0:T(1,128)S(1)} %add_bitcast_fusion), channel_id=1, replica_groups=mesh['slab'=32,'orb'=4] {'slab','orb'}, dimensions={0}, use_global_device_ids=true | all-gather | bytes 2580 | tf_op jit(solution)/shard_map/all_gather | solution.py:22
  151.4 6.2 %gather_fusion = f32[64,2,4096]{2,1,0:T(2,128)S(1)} fusion(f32[256,2,4096]{2,1,0:T(2,128)} %bitcast.16, s32[1024]{0:T(1024)S(1)} %pad_clamp_fusion), kind=kCustom, calls=%fused_computation | custom fusion | bytes 4194560 | tf_op jit(solution)/shard_map/jit(_take)/gather | solution.py:96
  157.6 2.4 gather.17
  160.0 1.9 select_select_fusion
  162.0 2.9 copy.27
  164.9 5.4 %all-to-all-start.1 = ((f32[1,2,64,4096]{3,1,0,2:T(2,128)}), f32[1,2,64,4096]{3,1,0,2:T(2,128)S(1)}, u32[]{:S(2)}, u32[]{:S(2)}) async-start(f32[1,2,64,4096]{3,1,0,2:T(2,128)} %copy.27), calls=%async_computation.1 | async-start | bytes 4194304 | tf_op jit(solution)/shard_map/all_to_all | solution.py:99
  170.4 28.5 %all-to-all-done.1 = f32[1,2,64,4096]{3,1,0,2:T(2,128)S(1)} async-done(((f32[1,2,64,4096]{3,1,0,2:T(2,128)}), f32[1,2,64,4096]{3,1,0,2:T(2,128)S(1)}, u32[]{:S(2)}, u32[]{:S(2)}) %all-to-all-start.1) | async-done | bytes 2097184 | tf_op jit(solution)/shard_map/all_to_all | solution.py:99
  198.9 2.3 broadcast_multiply_fusion
  202.5 54.3 %while.19 = (s32[]{:T(128)}, f32[1,64,4096]{2,1,0:T(8,128)S(1)}, f32[1,64,4096]{2,1,0:T(8,128)S(1)}, f32[1,64,4096]{2,1,0:T(8,128)S(1)}, f32[]{:T(128)}, /*index...) while((s32[]{:T(128)}, f32[1,64,4096]{2,1,0:T(8,128)S(1)}, ...), condition=%wide.region_1.2_spmd.clone, body=%wide.region_0.1_spmd.clone.sunk | while | flops 6062087 | bytes 32522424 | solution.py:51
  204.4 1.5 multiply_add_fusion.2
  207.8 1.5 multiply_add_fusion.2
  256.8 5.1 %fusion.13 = (f32[1,64,4096]{2,0,1:T(1,128)S(1)}, f32[1,64,4096]{2,0,1:T(1,128)S(1)}) fusion(f32[1,2,64,4096]{3,1,0,2:T(2,128)} %copy-done, f32[1,64,4096]{2,1,0:T(8,128)S(1)} %get-tuple-element.32), kind=kLoop, calls=%fused_computation.37 | loop fusion | flops 786432 | bytes 5242880 | tf_op jit(solution)/shard_map/mul | solution.py:58
  261.9 4.0 pad_maximum_fusion
  265.9 1.9 copy.46
  267.8 7.5 %broadcast_in_dim.91 = f32[2,32,4,2,4096]{4,0,3,2,1:T(2,128)} broadcast(f32[2,32,2,4096]{3,0,2,1:T(2,128)S(1)} %bitcast.59), dimensions={0,1,3,4} | broadcast | bytes 10485760 | tf_op jit(solution)/shard_map/broadcast_in_dim | solution.py:101
  275.3 6.4 %all-to-all-start.2 = ((f32[1,2,256,4096]{3,1,0,2:T(2,128)}), f32[1,2,256,4096]{3,1,0,2:T(2,128)}, u32[]{:S(2)}, u32[]{:S(2)}) async-start(f32[1,2,256,4096]{3,1,0,2:T(2,128)} %bitcast.56), calls=%async_computation.2 | async-start | bytes 16777216 | tf_op jit(solution)/shard_map/all_to_all | solution.py:106
  281.8 102.7 %all-to-all-done.2 = f32[1,2,256,4096]{3,1,0,2:T(2,128)} async-done(((f32[1,2,256,4096]{3,1,0,2:T(2,128)}), f32[1,2,256,4096]{3,1,0,2:T(2,128)}, u32[]{:S(2)}, u32[]{:S(2)}) %all-to-all-start.2) | async-done | bytes 8388640 | tf_op jit(solution)/shard_map/all_to_all | solution.py:106
  384.5 11.5 %copy.33 = f32[1,2,256,4096]{3,2,1,0:T(8,128)} copy(f32[1,2,256,4096]{3,1,0,2:T(2,128)} %all-to-all-done.2) | data formatting | bytes 16777216 | tf_op jit(solution)/shard_map/all_to_all | solution.py:106
  396.0 10.0 %reshape.593 = f32[256,8192]{1,0:T(8,128)} reshape(f32[1,2,256,4096]{3,2,1,0:T(8,128)} %copy.33) | data formatting | bytes 16777216 | tf_op jit(solution)/shard_map/reshape | solution.py:113
  406.0 9.0 %copy.34 = f32[8192,256]{1,0:T(8,128)} copy(f32[8192,256]{0,1:T(8,128)} %bitcast.58) | data formatting | bytes 16777216 | tf_op jit(solution)/shard_map/dot_general | solution.py:111
  415.0 7.7 %fusion.20 = f32[64,2,4096]{2,0,1:T(8,128)S(1)} fusion(f32[2,4096,256]{2,1,0:T(8,128)} %bitcast.57, s32[256]{0:T(256)S(1)} %bitcast.66), kind=kOutput, calls=%fused_computation.48 | convolution fusion | flops 1610629120 | bytes 10486784 | tf_op jit(solution)/shard_map/dot_general | solution.py:111
  422.7 2.9 copy.35
  (208 shorter events, 53.9 us)
Async XLA Ops:
  9.1 6.0 %copy-start.1 = (s32[1,3]{1,0:T(1,128)S(1)}, s32[1,3]{1,0:T(1,128)}, u32[]{:S(2)}) copy-start(s32[1,3]{1,0:T(1,128)} %param.7) | copy-start | bytes 40
  9.1 6.0 %copy-start.2 = (s32[1,2]{1,0:T(1,128)S(1)}, s32[1,2]{1,0:T(1,128)}, u32[]{:S(2)}) copy-start(s32[1,2]{1,0:T(1,128)} %param.6) | copy-start | bytes 28
  9.1 142.3 %all-to-all-start = ((f32[4,64,2,4096]{3,2,1,0:T(2,128)}), f32[4,64,2,4096]{3,2,1,0:T(2,128)}, u32[]{:S(2)}, u32[]{:S(2)}) async-start(f32[4,64,2,4096]{3,2,1,0:T(2,128)} %stack.16), calls=%async_computation | async-start | bytes 16777216 | tf_op jit(solution)/shard_map/all_to_all | solution.py:88
  164.9 34.0 %all-to-all-start.1 = ((f32[1,2,64,4096]{3,1,0,2:T(2,128)}), f32[1,2,64,4096]{3,1,0,2:T(2,128)S(1)}, u32[]{:S(2)}, u32[]{:S(2)}) async-start(f32[1,2,64,4096]{3,1,0,2:T(2,128)} %copy.27), calls=%async_computation.1 | async-start | bytes 4194304 | tf_op jit(solution)/shard_map/all_to_all | solution.py:99
  198.9 2.3 copy-start
  275.3 109.2 %all-to-all-start.2 = ((f32[1,2,256,4096]{3,1,0,2:T(2,128)}), f32[1,2,256,4096]{3,1,0,2:T(2,128)}, u32[]{:S(2)}, u32[]{:S(2)}) async-start(f32[1,2,256,4096]{3,1,0,2:T(2,128)} %bitcast.56), calls=%async_computation.2 | async-start | bytes 16777216 | tf_op jit(solution)/shard_map/all_to_all | solution.py:106
